TPU v7x, 256 devices: a whole 4x4x8 slice. The times are simulated.
256 devices in a mesh: cache: 32 (over x, z), owner: 8 (over y, core).
Axes of the slice: x: 4, y: 4, z: 8, core: 2. Of those that a mesh axis runs over, the one named last changes fastest.
Arguments:
- cache: bfloat16 [32, 4, 128, 256], P('cache'), may hold values from -2.5 to 2.5
- backing: bfloat16 [32, 64, 128, 256], P('cache', 'owner'), may hold values from -2.5 to 2.5
- resident: int32 [32, 4], P('cache'), may hold values from 0 to 63, as said below
- promote: int32 [32, 2], P('cache'), may hold values from 0 to 63, as said below
- victim: int32 [32, 2], P('cache'), may hold values from 0 to 3, as said below
- lookups: int32 [2, 32768, 32, 8], P(None, 'owner', 'cache'), may hold values from 0 to 511
- route: int32 [2, 8, 4096], P(None, 'owner'), may hold values from 0 to 4095, each once within a row
- dcn_down: bfloat16 [8192, 128], P('cache'), may hold values from -0.0625 to 0.0625
- dcn_up: bfloat16 [128, 8192], P(None, 'cache'), may hold values from -0.5 to 0.5
- dcn_bias: float32 [8192], replicated, may hold values from -5 to 5
- mlp_in: bfloat16 [8192, 1024], P('cache'), may hold values from -0.0625 to 0.0625
- mlp_bias: float32 [1024], replicated, may hold values from -3 to 3
- mlp_out: float32 [1024], replicated, may hold values from -0.1875 to 0.1875
- out_bias: float32 [1], replicated, may hold values from -4 to 4
Outputs:
- scores: float32 [2, 8, 4096], P(None, 'owner', 'cache')
- new_cache: bfloat16 [32, 4, 128, 256], P('cache')
- new_backing: bfloat16 [32, 64, 128, 256], P('cache', 'owner')
Inputs may be any that keep to these rules, and one draw needn't show every extreme that they name: `resident`: for each feature, 4 distinct backing blocks. `promote`: for each feature, 2 distinct backing blocks, none of them in that feature's resident; block k belongs to owner k // 8. `victim`: for each feature, 2 distinct slots. `route`: each batch and owner group holds every request index once.
All inputs are finite; a program needn't handle non-finite values.
Results may differ from a plain program's by a relative error of at most 0.004.
Values may be sent and summed in bfloat16 or wider, within the bound.
No kernel may reach another device: no remote copies, remote signals or barrier semaphores. Data moves between devices by JAX's collectives and lax.ppermute only.
A program may use at most 128 MiB of HBM per device.

v0:
```python
import jax
import jax.numpy as jnp
from jax import lax
from jax.sharding import PartitionSpec as P


def copy_for_each(x, axis):
    size = lax.axis_size(axis)
    return lax.all_to_all(jnp.broadcast_to(x[None], (size, *x.shape)), axis, 0, 0, tiled=True)


def in_order(blocks, dim):
    lengths = list(blocks.shape[1:])
    lengths[dim] *= blocks.shape[0]
    return jnp.moveaxis(blocks, 0, dim).reshape(lengths)


def gathered_copies(x, axis, dim):
    blocks = copy_for_each(x, axis)
    return in_order(blocks, dim)


def take_rows(table, wanted):
    return jax.vmap(lambda rows, chosen: rows[chosen])(table, wanted)


def pool_batch(requests, order, table):
    requests = requests[order]
    count = requests.shape[0]
    step = min(512, count)
    codes = jnp.arange(table.shape[1], dtype=jnp.int32)

    def one_block(lookup_block):
        counts = jnp.sum((lookup_block[..., None] == codes).astype(jnp.bfloat16), axis=2)
        return jnp.einsum("rfk,fke->rfe", counts, table, preferred_element_type=jnp.float32).astype(
            jnp.bfloat16
        )

    blocks = requests.reshape((count // step, step) + requests.shape[1:])
    pooled = lax.map(one_block, blocks)
    return pooled.reshape((count,) + pooled.shape[2:])


def on_device(
    cache,
    backing,
    resident,
    promote,
    victim,
    lookups,
    route,
    dcn_down,
    dcn_up,
    dcn_bias,
    mlp_in,
    mlp_bias,
    mlp_out,
    out_bias,
):
    held = cache.shape[0]
    slots = cache.shape[1]
    block = cache.shape[2]
    width = cache.shape[3]
    own_blocks = backing.shape[1]
    promoted_count = promote.shape[1]
    owner_here = lax.axis_index("owner")
    local_index = promote - owner_here * own_blocks
    owned_here = (local_index >= 0) & (local_index < own_blocks)
    clamped = jnp.clip(local_index, 0, own_blocks - 1)
    fetched = take_rows(backing, clamped)
    outgoing = jnp.where(owned_here[:, :, None, None], fetched, jnp.zeros_like(fetched))
    arrived = gathered_copies(outgoing, "owner", 0)
    owners = arrived.shape[0] // held
    arrived = arrived.reshape(owners, held, promoted_count, block, width)
    source = promote // own_blocks
    picked = source[None] == jnp.arange(owners, dtype=jnp.int32)[:, None, None]
    promoted = jnp.sum(jnp.where(picked[..., None, None], arrived, jnp.zeros_like(arrived)), axis=0)
    evicted = take_rows(cache, victim)
    leaving = take_rows(resident, victim) - owner_here * own_blocks
    slot_numbers = jnp.arange(slots, dtype=jnp.int32)
    block_numbers = jnp.arange(own_blocks, dtype=jnp.int32)
    new_cache = cache
    new_backing = backing
    for column in range(promoted_count):
        slot_hit = victim[:, column][:, None] == slot_numbers[None, :]
        new_cache = jnp.where(slot_hit[:, :, None, None], promoted[:, column][:, None], new_cache)
        block_hit = leaving[:, column][:, None] == block_numbers[None, :]
        new_backing = jnp.where(
            block_hit[:, :, None, None], evicted[:, column][:, None], new_backing
        )
    table = new_cache.reshape(held, slots * block, width)
    batches = lookups.shape[0]
    received = []
    for batch_turn in range(batches):
        pooled = pool_batch(lookups[batch_turn], route[batch_turn, 0], table)
        received.append(lax.all_to_all(pooled, "cache", split_axis=0, concat_axis=1, tiled=True))
    arrived_rows = jnp.stack(received)
    per_batch = arrived_rows.shape[1]
    features = arrived_rows.reshape(batches * per_batch, -1)
    columns = features
    low = jnp.dot(
        columns,
        lax.all_gather(dcn_down, "cache", axis=0, tiled=True),
        preferred_element_type=jnp.float32,
    ).astype(jnp.bfloat16)
    gate = (
        jnp.dot(
            low,
            lax.all_gather(dcn_up, "cache", axis=1, tiled=True),
            preferred_element_type=jnp.float32,
        )
        + dcn_bias
    )
    crossed = (features * gate + features).astype(jnp.bfloat16)
    columns = crossed
    before = jnp.dot(
        columns,
        lax.all_gather(mlp_in, "cache", axis=0, tiled=True),
        preferred_element_type=jnp.float32,
    )
    hidden = jnp.maximum(before + mlp_bias, 0.0)
    scores = jnp.sum(hidden * mlp_out, axis=-1) + out_bias[0]
    return (scores.reshape(batches, 1, per_batch), new_cache, new_backing)


def solution(mesh):
    in_specs = (
        P("cache", None, None, None),
        P("cache", "owner", None, None),
        P("cache", None),
        P("cache", None),
        P("cache", None),
        P(None, "owner", "cache", None),
        P(None, "owner", None),
        P("cache", None),
        P(None, "cache"),
        P(),
        P("cache", None),
        P(),
        P(),
        P(),
    )
    out_specs = (
        P(None, "owner", "cache"),
        P("cache", None, None, None),
        P("cache", "owner", None, None),
    )
    return jax.shard_map(
        on_device, mesh=mesh, in_specs=in_specs, out_specs=out_specs, check_vma=False
    )
```

profile of v0, /device:TPU:1, one launch (start us, length us, event | category | flops | bytes accessed | tf_op | source)
XLA Modules:
  0.0 363.3 jit_solution(7484960167387886002)
XLA Ops:
  10.4 1.6 gather_fusion.2
  12.8 1.1 broadcast_in_dim.137
  13.9 6.7 %all-to-all-start = ((bf16[8,1,2,128,256]{4,3,2,1,0:T(8,128)(2,1)}), bf16[8,1,2,128,256]{4,3,2,1,0:T(8,128)(2,1)S(1)}, u32[]{:S(2)}, u32[]{:S(2)}) async-start(bf16[8,1,2,128,256]{4,3,2,1,0:T(8,128)(2,1)} %broadcast_in_dim.137), calls=%async_computation | async-start | bytes 2097152 | tf_op jit(solution)/shard_map/all_to_all | solution.py:9
  21.2 14.1 %gather_fusion = s32[4096,8]{1,0:T(8,128)} fusion(s32[4096,8]{1,0:T(8,128)S(1)} %bitcast.111, s32[4096]{0:T(1024)S(1)} %broadcast_clamp_fusion.1), kind=kCustom, calls=%fused_computation | custom fusion | bytes 278528 | tf_op jit(solution)/shard_map/gather | solution.py:28
  35.4 2.8 copy.64
  38.8 14.1 %gather_fusion.1 = s32[4096,8]{1,0:T(8,128)} fusion(s32[4096,8]{1,0:T(8,128)S(1)} %bitcast.110, s32[4096]{0:T(1024)S(1)} %broadcast_clamp_fusion), kind=kCustom, calls=%fused_computation.1 | custom fusion | bytes 278528 | tf_op jit(solution)/shard_map/gather | solution.py:28
  52.9 2.2 copy.67
  55.8 1.3 iota_compare_fusion.5
  57.6 35.3 %while.26 = (s32[]{:T(128)}, bf16[8,512,1,256]{3,1,2,0:T(8,128)(2,1)S(1)}, s32[8,512,1,8]{1,3,2,0:T(8,128)}, bf16[1,512,256]{2,1,0:T(8,128)(2,1)S(1)}, s32[]{:T(128)}) while((s32[]{:T(128)}, bf16[8,512,1,256]{3,1,2,0:T(8,128)(2,1)S(1)}, s32[8,512,1,8]{1,3,2,0:T(8,128)}, bf16[1,512,256]{2,1,0:T(8,128)(2,1)S(1)}, s32[]{:T(128)}) %tuple.90), condition=%wide.region_3.4_spmd.clone, body=%wide.region_1.3_spmd.clone.sunk | while | flops 140378112 | bytes 1654853 | solution.py:40
  58.4 3.2 fusion.41
  62.8 3.2 fusion.41
  67.2 3.2 fusion.41
  71.7 3.2 fusion.41
  76.1 3.2 fusion.41
  80.5 3.2 fusion.41
  84.9 3.2 fusion.41
  89.3 3.2 fusion.41
  93.4 2.9 reduce.17
  96.3 4.0 %reshape.321 = bf16[32,2,16384]{2,1,0:T(2,128)(2,1)} reshape(bf16[4096,256]{1,0:T(8,128)(2,1)} %reduce.17) | data formatting | bytes 4194304
  100.3 10.3 %all-to-all-start.1 = ((bf16[32,2,16384]{2,1,0:T(2,128)(2,1)}), bf16[32,2,16384]{2,1,0:T(2,128)(2,1)S(1)}, u32[]{:S(2)}, u32[]{:S(2)}) async-start(bf16[32,2,16384]{2,1,0:T(2,128)(2,1)} %reshape.321), calls=%async_computation.1 | async-start | bytes 4194304 | tf_op jit(solution)/shard_map/all_to_all | solution.py:96
  110.6 1.5 broadcast.187.clone
  112.1 35.1 %while.27 = (s32[]{:T(128)}, bf16[8,512,1,256]{3,1,2,0:T(8,128)(2,1)}, s32[8,512,1,8]{1,3,2,0:T(8,128)S(1)}, bf16[1,512,256]{2,1,0:T(8,128)(2,1)S(1)}, s32[]{:T(128)}) while((s32[]{:T(128)}, bf16[8,512,1,256]{3,1,2,0:T(8,128)(2,1)}, s32[8,512,1,8]{1,3,2,0:T(8,128)S(1)}, bf16[1,512,256]{2,1,0:T(8,128)(2,1)S(1)}, s32[]{:T(128)}) %tuple.91), condition=%wide.region_6.7_spmd.clone, body=%wide.region_4.6_spmd.clone.sunk | while | flops 140378112 | bytes 1655361 | solution.py:40
  112.2 3.2 fusion.45
  115.5 1.0 fusion.46
  116.6 3.2 fusion.45
  119.9 1.0 fusion.46
  121.0 3.2 fusion.45
  124.3 1.0 fusion.46
  125.4 3.2 fusion.45
  129.8 3.2 fusion.45
  134.2 3.2 fusion.45
  138.6 3.2 fusion.45
  143.0 3.2 fusion.45
  147.2 4.5 %reduce.16 = bf16[4096,256]{1,0:T(8,128)(2,1)} reduce(bf16[4096,1,256]{2,0,1:T(8,128)(2,1)} %bitcast.116, bf16[]{:T(256)} %broadcast.259), dimensions={1}, to_apply=%copy.68.reduce_sub_computation | reduce | bytes 4194306 | tf_op jit(solution)/shard_map/reshape | solution.py:41
  151.7 4.0 %reshape.319 = bf16[32,2,16384]{2,1,0:T(2,128)(2,1)} reshape(bf16[4096,256]{1,0:T(8,128)(2,1)} %reduce.16) | data formatting | bytes 4194304
  155.7 6.3 %all-to-all-done.1 = bf16[32,2,16384]{2,1,0:T(2,128)(2,1)S(1)} async-done(((bf16[32,2,16384]{2,1,0:T(2,128)(2,1)}), bf16[32,2,16384]{2,1,0:T(2,128)(2,1)S(1)}, u32[]{:S(2)}, u32[]{:S(2)}) %all-to-all-start.1) | async-done | bytes 2097184 | tf_op jit(solution)/shard_map/all_to_all | solution.py:96
  162.0 10.4 %all-to-all-start.2 = ((bf16[32,2,16384]{2,1,0:T(2,128)(2,1)}), bf16[32,2,16384]{2,1,0:T(2,128)(2,1)}, u32[]{:S(2)}, u32[]{:S(2)}) async-start(bf16[32,2,16384]{2,1,0:T(2,128)(2,1)} %reshape.319), calls=%async_computation.2 | async-start | bytes 4194304 | tf_op jit(solution)/shard_map/all_to_all | solution.py:96
  175.2 1.3 iota_compare_fusion.3
  177.5 6.7 %reshape.322 = bf16[4096,1,256]{2,1,0:T(2,128)(2,1)} reshape(bf16[32,2,16384]{2,1,0:T(2,128)(2,1)S(1)} %all-to-all-done.1) | data formatting | bytes 4194304
  184.2 2.5 copy.71
  186.8 41.1 %all-to-all-done.2 = bf16[32,2,16384]{2,1,0:T(2,128)(2,1)} async-done(((bf16[32,2,16384]{2,1,0:T(2,128)(2,1)}), bf16[32,2,16384]{2,1,0:T(2,128)(2,1)}, u32[]{:S(2)}, u32[]{:S(2)}) %all-to-all-start.2) | async-done | bytes 2097184 | tf_op jit(solution)/shard_map/all_to_all | solution.py:96
  227.9 10.4 %reshape.320 = bf16[4096,1,256]{2,1,0:T(2,128)(2,1)} reshape(bf16[32,2,16384]{2,1,0:T(2,128)(2,1)} %all-to-all-done.2) | data formatting | bytes 4194304
  238.3 2.6 copy.72
  241.3 2.4 copy.69
  243.7 6.2 %copy.77 = bf16[32,8,32,256]{3,1,2,0:T(8,128)(2,1)} copy(bf16[32,8,32,256]{3,2,1,0:T(8,128)(2,1)S(1)} %bitcast.114) | data formatting | bytes 8388608
  249.9 4.1 %convolution_convert_fusion.2 = bf16[256,128]{1,0:T(8,128)(2,1)S(1)} fusion(bf16[256,8192]{1,0:T(8,128)(2,1)} %bitcast.112, bf16[8192,128]{1,0:T(8,128)(2,1)} %all-gather.4.cloned.1.call-done), kind=kOutput, calls=%fused_computation.31 | convolution fusion | flops 536903680 | bytes 6356992 | tf_op jit(solution)/shard_map/dot_general | solution.py:101
  254.1 89.4 %all-gather.8.cloned.1.call-done = bf16[8192,1024]{1,0:T(8,128)(2,1)} async-done(((bf16[256,1024]{1,0:T(8,128)(2,1)}), bf16[8192,1024]{1,0:T(8,128)(2,1)}) %all-gather.8.cloned.1.call-update) | async-done | bytes 16777232 | tf_op jit(solution)/shard_map/all_gather | solution.py:118
  343.5 12.7 %fusion.17 = f32[256]{0:T(256)S(1)} fusion(bf16[8192,1024]{1,0:T(8,128)(2,1)} %all-gather.8.cloned.1.call-done, bf16[256,128]{1,0:T(8,128)(2,1)S(1)} %convolution_convert_fusion.2, bf16[128,8192]{1,0:T(8,128)(2,1)} %all-gather.6.cloned.1.call-done, bf16[256,8192]{1,0:T(8,128)(2,1)} %bitcast.113, f32[8192]{0:T(1024)S(1)} %copy-done.8, ...), kind=kOutput, calls=%fused_computation.30 | convolution fusion | flops 4843372544 | bytes 23176192 | tf_op jit(solution)/shard_map/dot_general | solution.py:116
  (107 shorter events, 26.2 us)
Async XLA Ops:
  7.2 166.8 %copy-start = (s32[1,4]{1,0:T(1,128)S(1)}, s32[1,4]{1,0:T(1,128)}, u32[]{:S(2)}) copy-start(s32[1,4]{1,0:T(1,128)} %param.20) | copy-start | bytes 52
  7.2 242.7 %all-gather.4.cloned.1.call-start = ((), (), s32[]{:S(2)}) async-start(), calls=%async_computation.3 | async-start | bytes 2162688 | tf_op jit(solution)/shard_map/all_gather | solution.py:103
  7.9 246.2 %all-gather.6.cloned.1.call-start = ((), (), s32[]{:S(2)}) async-start(), calls=%async_computation.4 | async-start | bytes 2162688 | tf_op jit(solution)/shard_map/all_gather | solution.py:109
  8.7 11.9 %copy-start.5 = (s32[2,4096,1,8]{1,3,2,0:T(8,128)S(1)}, s32[2,4096,1,8]{1,3,2,0:T(8,128)}, u32[]{:S(2)}) copy-start(s32[2,4096,1,8]{1,3,2,0:T(8,128)} %param.23) | copy-start | bytes 786436
  8.7 334.8 %all-gather.8.cloned.1.call-start = ((), (), s32[]{:S(2)}) async-start(), calls=%async_computation.5 | async-start | bytes 17301504 | tf_op jit(solution)/shard_map/all_gather | solution.py:118
  12.0 8.5 %copy-start.6 = (s32[2,1,4096]{2,1,0:T(1,128)S(1)}, s32[2,1,4096]{2,1,0:T(1,128)}, u32[]{:S(2)}) copy-start(s32[2,1,4096]{2,1,0:T(1,128)} %param.24) | copy-start | bytes 98308
  13.9 43.2 %all-to-all-start = ((bf16[8,1,2,128,256]{4,3,2,1,0:T(8,128)(2,1)}), bf16[8,1,2,128,256]{4,3,2,1,0:T(8,128)(2,1)S(1)}, u32[]{:S(2)}, u32[]{:S(2)}) async-start(bf16[8,1,2,128,256]{4,3,2,1,0:T(8,128)(2,1)} %broadcast_in_dim.137), calls=%async_computation | async-start | bytes 2097152 | tf_op jit(solution)/shard_map/all_to_all | solution.py:9
  52.9 2.2 copy-start.7
  52.9 4.4 %copy-start.3 = (bf16[1,4,128,256]{3,2,1,0:T(8,128)(2,1)S(1)}, bf16[1,4,128,256]{3,2,1,0:T(8,128)(2,1)}, u32[]{:S(2)}) copy-start(bf16[1,4,128,256]{3,2,1,0:T(8,128)(2,1)} %param.18) | copy-start | bytes 786436
  100.3 61.7 %all-to-all-start.1 = ((bf16[32,2,16384]{2,1,0:T(2,128)(2,1)}), bf16[32,2,16384]{2,1,0:T(2,128)(2,1)S(1)}, u32[]{:S(2)}, u32[]{:S(2)}) async-start(bf16[32,2,16384]{2,1,0:T(2,128)(2,1)} %reshape.321), calls=%async_computation.1 | async-start | bytes 4194304 | tf_op jit(solution)/shard_map/all_to_all | solution.py:96
  147.2 4.5 %copy-start.4 = (bf16[1,512,256]{2,1,0:T(8,128)(2,1)}, bf16[1,512,256]{2,1,0:T(8,128)(2,1)S(1)}, u32[]{:S(2)}) copy-start(bf16[1,512,256]{2,1,0:T(8,128)(2,1)S(1)} %get-tuple-element.330) | copy-start | bytes 786436
  155.7 20.8 %copy-start.2 = (bf16[1,8,128,256]{3,2,1,0:T(8,128)(2,1)S(1)}, bf16[1,8,128,256]{3,2,1,0:T(8,128)(2,1)}, u32[]{:S(2)}) copy-start(bf16[1,8,128,256]{3,2,1,0:T(8,128)(2,1)} %param.19) | copy-start | bytes 1572868
  162.0 65.9 %all-to-all-start.2 = ((bf16[32,2,16384]{2,1,0:T(2,128)(2,1)}), bf16[32,2,16384]{2,1,0:T(2,128)(2,1)}, u32[]{:S(2)}, u32[]{:S(2)}) async-start(bf16[32,2,16384]{2,1,0:T(2,128)(2,1)} %reshape.319), calls=%async_computation.2 | async-start | bytes 4194304 | tf_op jit(solution)/shard_map/all_to_all | solution.py:96
  249.9 93.6 %copy-start.8 = (f32[8192]{0:T(1024)S(1)}, f32[8192]{0:T(1024)}, u32[]{:S(2)}) copy-start(f32[8192]{0:T(1024)} %param.27) | copy-start | bytes 98308
  249.9 93.6 %copy-start.9 = (f32[1024]{0:T(1024)S(1)}, f32[1024]{0:T(1024)}, u32[]{:S(2)}) copy-start(f32[1024]{0:T(1024)} %param.30) | copy-start | bytes 12292
  249.9 93.6 %copy-start.10 = (f32[1024]{0:T(1024)S(1)}, f32[1024]{0:T(1024)}, u32[]{:S(2)}) copy-start(f32[1024]{0:T(1024)} %param.29) | copy-start | bytes 12292
  343.5 13.2 %copy-start.1 = (s32[1,4]{1,0:T(1,128)S(1)}, s32[1,4]{1,0:T(1,128)}, u32[]{:S(2)}) copy-start(s32[1,4]{1,0:T(1,128)} %param.20) | copy-start | bytes 52
Sparse Core Ops, SparseCore 0:
  10.6 77.0 all-gather.3
  90.1 95.1 all-gather.5
  187.9 155.6 all-gather.7
where the time goes:
time: 365 us; the launch traced here: 363 us
  waiting for transfers between devices  139 us (38%)
  local copies, waits for them, and re-layouts  88.8 us (24%)
  other arithmetic  65.7 us (18%)
  starting transfers between devices  27.5 us (8%)
  matrix products  27.3 us (7%)
  between operations  14.7 us (4%)
    all_gather x1, waiting for transfers between devices, on_device(): lax.all_gather(mlp_in, 'cache', axis=0, tiled=True)  89.4 us
    reduce_sum x16, other arithmetic, one_block(): jnp.sum((lookup_block[..., None] == codes).astype(jnp.bfloat16), axis=2)  51.7 us
    all_to_all x2, waiting for transfers between devices, on_device(): lax.all_to_all(pooled, 'cache', split_axis=0, concat_axis=1, tiled=True)  47.4 us
    unnamed x35, local copies, waits for them, and re-layouts  42.9 us
    gather x2, local copies, waits for them, and re-layouts, pool_batch(): requests = requests[order]  28.2 us
    all_to_all x2, starting transfers between devices, on_device(): lax.all_to_all(pooled, 'cache', split_axis=0, concat_axis=1, tiled=True)  20.7 us
    dot_general x1, matrix products, on_device(): jnp.dot(columns, lax.all_gather(mlp_in, 'cache', axis=0, tiled=True), pre...  12.7 us
    dot_general x16, matrix products, one_block(): jnp.einsum('rfk,fke->rfe', counts, table, preferred_element_type=jnp.floa...  10.5 us
  transfers between devices with their start and end apart: 6, of which 3 were waited for; matrix products, arithmetic and copies ran while one was open for 46% of the time, Pallas kernels for 0%

commit v1 on v0

--- a/solution.py
+++ b/solution.py
@@ -93,7 +93,14 @@
     received = []
     for batch_turn in range(batches):
         pooled = pool_batch(lookups[batch_turn], route[batch_turn, 0], table)
-        received.append(lax.all_to_all(pooled, "cache", split_axis=0, concat_axis=1, tiled=True))
+        received.append(
+            jnp.concatenate(
+                lax.all_to_all(
+                    jnp.stack(jnp.split(pooled, lax.axis_size("cache"), axis=0)), "cache", 0, 0
+                ),
+                axis=1,
+            )
+        )
     arrived_rows = jnp.stack(received)
     per_batch = arrived_rows.shape[1]
     features = arrived_rows.reshape(batches * per_batch, -1)

time: 365 us -> 373 us (1.022)
  waiting for transfers between devices: 139 us -> 153 us
  local copies, waits for them, and re-layouts: 88.8 us -> 96.5 us
  other arithmetic: 65.7 us -> 59.9 us
  matrix products: 27.3 us -> 21.6 us
    all_to_all x2, waiting for transfers between devices: 47.4 us -> 56.4 us  [on_device(): lax.all_to_all(jnp.stack(jnp.split(pooled, lax.axis_size('cache'), axis=0...]
    unnamed x35 -> x89, local copies, waits for them, and re-layouts: 42.9 us -> 51.3 us
    reshape x2 -> x0, other arithmetic: 7.43 us -> none  [pool_batch(): return pooled.reshape((count,) + pooled.shape[2:])]
    dot_general x16, matrix products: 10.5 us -> 4.79 us  [one_block(): jnp.einsum('rfk,fke->rfe', counts, table, preferred_element_type=jnp.floa...]
    all_gather x1, waiting for transfers between devices: 89.4 us -> 94.1 us  [on_device(): lax.all_gather(mlp_in, 'cache', axis=0, tiled=True)]
  transfers between devices with their start and end apart: 6 -> 6, of which waited for: 3 -> 3; matrix products, arithmetic and copies ran while one was open for 46% -> 44% of each run, Pallas kernels for 0% -> 0%
where the time goes in v1:
time: 373 us; the launch traced here: 372 us
  waiting for transfers between devices  153 us (41%)
  local copies, waits for them, and re-layouts  96.5 us (26%)
  other arithmetic  59.9 us (16%)
  starting transfers between devices  26.2 us (7%)
  matrix products  21.6 us (6%)
  between operations  14.7 us (4%)
    all_gather x1, waiting for transfers between devices, on_device(): lax.all_gather(mlp_in, 'cache', axis=0, tiled=True)  94.1 us
    all_to_all x2, waiting for transfers between devices, on_device(): lax.all_to_all(jnp.stack(jnp.split(pooled, lax.axis_size('cache'), axis=0...  56.4 us
    reduce_sum x16, other arithmetic, one_block(): jnp.sum((lookup_block[..., None] == codes).astype(jnp.bfloat16), axis=2)  51.7 us
    unnamed x89, local copies, waits for them, and re-layouts  51.3 us
    gather x2, local copies, waits for them, and re-layouts, pool_batch(): requests = requests[order]  28.2 us
    all_to_all x2, starting transfers between devices, on_device(): lax.all_to_all(jnp.stack(jnp.split(pooled, lax.axis_size('cache'), axis=0...  19.5 us
    dot_general x1, matrix products, on_device(): jnp.dot(columns, lax.all_gather(mlp_in, 'cache', axis=0, tiled=True), pre...  12.7 us
    eq x32, local copies, waits for them, and re-layouts, one_block(): lookup_block[..., None] == codes  7.82 us
  transfers between devices with their start and end apart: 6, of which 3 were waited for; matrix products, arithmetic and copies ran while one was open for 44% of the time, Pallas kernels for 0%

profile of v1, /device:TPU:1, one launch (start us, length us, event | category | flops | bytes accessed | tf_op | source)
XLA Modules:
  0.0 372.1 jit_solution(443925231839151901)
XLA Ops:
  7.2 0.7 all-gather.4.cloned.1.call-update
  8.0 0.7 all-gather.6.cloned.1.call-update
  10.4 1.6 gather_fusion.2
  12.8 1.1 broadcast_in_dim.137
  13.9 6.7 %all-to-all-start = ((bf16[8,1,2,128,256]{4,3,2,1,0:T(8,128)(2,1)}), bf16[8,1,2,128,256]{4,3,2,1,0:T(8,128)(2,1)S(1)}, u32[]{:S(2)}, u32[]{:S(2)}) async-start(bf16[8,1,2,128,256]{4,3,2,1,0:T(8,128)(2,1)} %broadcast_in_dim.137), calls=%async_computation | async-start | bytes 2097152 | tf_op jit(solution)/shard_map/all_to_all | solution.py:9
  21.2 14.1 %gather_fusion = s32[4096,8]{1,0:T(8,128)} fusion(s32[4096,8]{1,0:T(8,128)S(1)} %bitcast.364, s32[4096]{0:T(1024)S(1)} %get-tuple-element.226), kind=kCustom, calls=%fused_computation | custom fusion | bytes 278528 | tf_op jit(solution)/shard_map/gather | solution.py:28
  35.3 2.8 copy.178
  38.8 14.1 %gather_fusion.1 = s32[4096,8]{1,0:T(8,128)} fusion(s32[4096,8]{1,0:T(8,128)S(1)} %bitcast.365, s32[4096]{0:T(1024)S(1)} %get-tuple-element.225), kind=kCustom, calls=%fused_computation.1 | custom fusion | bytes 278528 | tf_op jit(solution)/shard_map/gather | solution.py:28
  52.8 2.2 copy.180
  55.7 1.2 iota_compare_fusion.5
  57.5 35.3 %while.26 = (s32[]{:T(128)}, bf16[8,512,1,256]{3,1,2,0:T(8,128)(2,1)S(1)}, s32[8,512,1,8]{1,3,2,0:T(8,128)}, bf16[1,512,256]{2,1,0:T(8,128)(2,1)S(1)}, s32[]{:T(128)}) while((s32[]{:T(128)}, bf16[8,512,1,256]{3,1,2,0:T(8,128)(2,1)S(1)}, s32[8,512,1,8]{1,3,2,0:T(8,128)}, bf16[1,512,256]{2,1,0:T(8,128)(2,1)S(1)}, s32[]{:T(128)}) %tuple.89), condition=%wide.region_3.4_spmd.clone, body=%wide.region_1.3_spmd.clone.sunk | while | flops 140378112 | bytes 1654853 | solution.py:40
  57.5 0.7 dynamic-slice_bitcast_fusion.4
  58.4 3.2 fusion.41
  61.9 0.7 dynamic-slice_bitcast_fusion.4
  62.8 3.2 fusion.41
  66.3 0.7 dynamic-slice_bitcast_fusion.4
  67.2 3.2 fusion.41
  70.7 0.7 dynamic-slice_bitcast_fusion.4
  71.6 3.2 fusion.41
  75.2 0.7 dynamic-slice_bitcast_fusion.4
  76.0 3.2 fusion.41
  79.6 0.7 dynamic-slice_bitcast_fusion.4
  80.4 3.2 fusion.41
  84.0 0.7 dynamic-slice_bitcast_fusion.4
  84.8 3.2 fusion.41
  88.4 0.7 dynamic-slice_bitcast_fusion.4
  89.2 3.2 fusion.41
  112.7 10.5 %all-to-all-start.1 = ((bf16[32,128,1,256]{3,1,2,0:T(8,128)(2,1)}), bf16[32,128,1,256]{3,1,2,0:T(8,128)(2,1)}, u32[]{:S(2)}, u32[]{:S(2)}) async-start(bf16[32,128,1,256]{3,1,2,0:T(8,128)(2,1)} %constant_dynamic-update-slice_fusion), calls=%async_computation.1 | async-start | bytes 4194304 | tf_op jit(solution)/shard_map/all_to_all | solution.py:98
  123.3 29.6 %while.27 = (s32[]{:T(128)}, bf16[8,512,1,256]{3,1,2,0:T(8,128)(2,1)S(1)}, s32[8,512,1,8]{1,3,2,0:T(8,128)S(1)}, bf16[1,512,256]{2,1,0:T(8,128)(2,1)S(1)}, s32[]{:T(128)}) while((s32[]{:T(128)}, bf16[8,512,1,256]{3,1,2,0:T(8,128)(2,1)S(1)}, s32[8,512,1,8]{1,3,2,0:T(8,128)S(1)}, bf16[1,512,256]{2,1,0:T(8,128)(2,1)S(1)}, ...), condition=%wide.region_6.7_spmd.clone, body=%wide.region_4.6_spmd.clone.sunk | while | flops 140378112 | bytes 1654853 | solution.py:40
  123.5 3.2 fusion.45
  127.2 3.2 fusion.45
  130.9 3.2 fusion.45
  134.6 3.2 fusion.45
  138.3 3.2 fusion.45
  142.0 3.2 fusion.45
  145.7 3.2 fusion.45
  149.4 3.2 fusion.45
  172.9 4.3 %all-to-all-done.1 = bf16[32,128,1,256]{3,1,2,0:T(8,128)(2,1)} async-done(((bf16[32,128,1,256]{3,1,2,0:T(8,128)(2,1)}), bf16[32,128,1,256]{3,1,2,0:T(8,128)(2,1)}, u32[]{:S(2)}, u32[]{:S(2)}) %all-to-all-start.1) | async-done | bytes 2097184 | tf_op jit(solution)/shard_map/all_to_all | solution.py:98
  177.2 9.0 %all-to-all-start.2 = ((bf16[32,128,1,256]{3,1,2,0:T(8,128)(2,1)}), bf16[32,128,1,256]{3,1,2,0:T(8,128)(2,1)S(1)}, u32[]{:S(2)}, u32[]{:S(2)}) async-start(bf16[32,128,1,256]{3,1,2,0:T(8,128)(2,1)} %constant_dynamic-update-slice_fusion.32), calls=%async_computation.2 | async-start | bytes 4194304 | tf_op jit(solution)/shard_map/all_to_all | solution.py:98
  189.1 1.3 iota_compare_fusion.3
  190.4 0.9 select_select_fusion
  191.3 52.0 %all-to-all-done.2 = bf16[32,128,1,256]{3,1,2,0:T(8,128)(2,1)S(1)} async-done(((bf16[32,128,1,256]{3,1,2,0:T(8,128)(2,1)}), bf16[32,128,1,256]{3,1,2,0:T(8,128)(2,1)S(1)}, u32[]{:S(2)}, u32[]{:S(2)}) %all-to-all-start.2) | async-done | bytes 2097184 | tf_op jit(solution)/shard_map/all_to_all | solution.py:98
  243.4 2.0 pad_maximum_fusion
  245.4 2.4 copy.182
  247.8 6.2 %copy.188 = bf16[32,8,32,256]{3,1,2,0:T(8,128)(2,1)} copy(bf16[32,8,32,256]{3,2,1,0:T(8,128)(2,1)S(1)} %bitcast.368) | data formatting | bytes 8388608
  254.0 4.1 %convolution_convert_fusion.2 = bf16[256,128]{1,0:T(8,128)(2,1)S(1)} fusion(bf16[256,8192]{1,0:T(8,128)(2,1)} %bitcast.366, bf16[8192,128]{1,0:T(8,128)(2,1)} %all-gather.4.cloned.1.call-done), kind=kOutput, calls=%fused_computation.31 | convolution fusion | flops 536903680 | bytes 6356992 | tf_op jit(solution)/shard_map/dot_general | solution.py:108
  258.2 94.1 %all-gather.8.cloned.1.call-done = bf16[8192,1024]{1,0:T(8,128)(2,1)} async-done(((bf16[256,1024]{1,0:T(8,128)(2,1)}), bf16[8192,1024]{1,0:T(8,128)(2,1)}) %all-gather.8.cloned.1.call-update) | async-done | bytes 16777232 | tf_op jit(solution)/shard_map/all_gather | solution.py:125
  352.3 12.7 %fusion.17 = f32[256]{0:T(256)S(1)} fusion(bf16[8192,1024]{1,0:T(8,128)(2,1)} %all-gather.8.cloned.1.call-done, bf16[256,128]{1,0:T(8,128)(2,1)S(1)} %convolution_convert_fusion.2, bf16[128,8192]{1,0:T(8,128)(2,1)} %all-gather.6.cloned.1.call-done, bf16[256,8192]{1,0:T(8,128)(2,1)} %bitcast.367, f32[8192]{0:T(1024)S(1)} %copy-done.7, ...), kind=kOutput, calls=%fused_computation.30 | convolution fusion | flops 4843372544 | bytes 23176192 | tf_op jit(solution)/shard_map/dot_general | solution.py:123
  (159 shorter events, 54.6 us)
Async XLA Ops:
  7.2 180.7 %copy-start = (s32[1,4]{1,0:T(1,128)S(1)}, s32[1,4]{1,0:T(1,128)}, u32[]{:S(2)}) copy-start(s32[1,4]{1,0:T(1,128)} %param.20) | copy-start | bytes 52
  7.2 246.8 %all-gather.4.cloned.1.call-start = ((), (), s32[]{:S(2)}) async-start(), calls=%async_computation.3 | async-start | bytes 2162688 | tf_op jit(solution)/shard_map/all_gather | solution.py:110
  7.9 250.3 %all-gather.6.cloned.1.call-start = ((), (), s32[]{:S(2)}) async-start(), calls=%async_computation.4 | async-start | bytes 2162688 | tf_op jit(solution)/shard_map/all_gather | solution.py:116
  8.7 11.9 %copy-start.4 = (s32[2,4096,1,8]{1,3,2,0:T(8,128)S(1)}, s32[2,4096,1,8]{1,3,2,0:T(8,128)}, u32[]{:S(2)}) copy-start(s32[2,4096,1,8]{1,3,2,0:T(8,128)} %param.23) | copy-start | bytes 786436
  8.7 343.6 %all-gather.8.cloned.1.call-start = ((), (), s32[]{:S(2)}) async-start(), calls=%async_computation.5 | async-start | bytes 17301504 | tf_op jit(solution)/shard_map/all_gather | solution.py:125
  12.0 8.5 %copy-start.5 = (s32[2,1,4096]{2,1,0:T(1,128)S(1)}, s32[2,1,4096]{2,1,0:T(1,128)}, u32[]{:S(2)}) copy-start(s32[2,1,4096]{2,1,0:T(1,128)} %param.24) | copy-start | bytes 98308
  13.9 43.1 %all-to-all-start = ((bf16[8,1,2,128,256]{4,3,2,1,0:T(8,128)(2,1)}), bf16[8,1,2,128,256]{4,3,2,1,0:T(8,128)(2,1)S(1)}, u32[]{:S(2)}, u32[]{:S(2)}) async-start(bf16[8,1,2,128,256]{4,3,2,1,0:T(8,128)(2,1)} %broadcast_in_dim.137), calls=%async_computation | async-start | bytes 2097152 | tf_op jit(solution)/shard_map/all_to_all | solution.py:9
  52.8 2.2 copy-start.6
  52.8 4.4 %copy-start.2 = (bf16[1,4,128,256]{3,2,1,0:T(8,128)(2,1)S(1)}, bf16[1,4,128,256]{3,2,1,0:T(8,128)(2,1)}, u32[]{:S(2)}) copy-start(bf16[1,4,128,256]{3,2,1,0:T(8,128)(2,1)} %param.18) | copy-start | bytes 786436
  112.7 64.5 %all-to-all-start.1 = ((bf16[32,128,1,256]{3,1,2,0:T(8,128)(2,1)}), bf16[32,128,1,256]{3,1,2,0:T(8,128)(2,1)}, u32[]{:S(2)}, u32[]{:S(2)}) async-start(bf16[32,128,1,256]{3,1,2,0:T(8,128)(2,1)} %constant_dynamic-update-slice_fusion), calls=%async_computation.1 | async-start | bytes 4194304 | tf_op jit(solution)/shard_map/all_to_all | solution.py:98
  152.9 20.0 %copy-start.3 = (bf16[1,512,256]{2,1,0:T(8,128)(2,1)}, bf16[1,512,256]{2,1,0:T(8,128)(2,1)S(1)}, u32[]{:S(2)}) copy-start(bf16[1,512,256]{2,1,0:T(8,128)(2,1)S(1)} %get-tuple-element.320) | copy-start | bytes 786436
  172.9 17.5 %copy-start.1 = (bf16[1,8,128,256]{3,2,1,0:T(8,128)(2,1)S(1)}, bf16[1,8,128,256]{3,2,1,0:T(8,128)(2,1)}, u32[]{:S(2)}) copy-start(bf16[1,8,128,256]{3,2,1,0:T(8,128)(2,1)} %param.19) | copy-start | bytes 1572868
  177.2 66.1 %all-to-all-start.2 = ((bf16[32,128,1,256]{3,1,2,0:T(8,128)(2,1)}), bf16[32,128,1,256]{3,1,2,0:T(8,128)(2,1)S(1)}, u32[]{:S(2)}, u32[]{:S(2)}) async-start(bf16[32,128,1,256]{3,1,2,0:T(8,128)(2,1)} %constant_dynamic-update-slice_fusion.32), calls=%async_computation.2 | async-start | bytes 4194304 | tf_op jit(solution)/shard_map/all_to_all | solution.py:98
  254.0 98.3 %copy-start.7 = (f32[8192]{0:T(1024)S(1)}, f32[8192]{0:T(1024)}, u32[]{:S(2)}) copy-start(f32[8192]{0:T(1024)} %param.27) | copy-start | bytes 98308
  254.0 98.3 %copy-start.8 = (f32[1024]{0:T(1024)S(1)}, f32[1024]{0:T(1024)}, u32[]{:S(2)}) copy-start(f32[1024]{0:T(1024)} %param.30) | copy-start | bytes 12292
  254.0 98.3 %copy-start.9 = (f32[1024]{0:T(1024)S(1)}, f32[1024]{0:T(1024)}, u32[]{:S(2)}) copy-start(f32[1024]{0:T(1024)} %param.29) | copy-start | bytes 12292
Sparse Core Ops, SparseCore 0:
  10.6 76.7 all-gather.3
  89.9 95.9 all-gather.5
  188.4 163.8 all-gather.7
